TPU v7x, 32 devices: a whole 2x2x4 slice. The times are simulated.
32 devices in a mesh: grp: 2 (over x), seq: 8 (over z, y), kv: 2 (over core).
Axes of the slice: x: 2, y: 2, z: 4, core: 2. Of those that a mesh axis runs over, the one named last changes fastest.
Arguments:
- queries: bfloat16 [4, 64, 128], P(('grp', 'kv'), 'seq'), parts along dimension 0, may hold values from -256 to 256
- keys: bfloat16 [4, 16384, 8, 128], P(('grp', 'kv'), 'seq'), parts along dimension 0, may hold values from -6 to 6
- values: bfloat16 [4, 16384, 8, 128], P(('grp', 'kv'), 'seq'), parts along dimension 0, may hold values from -6 to 6
- picks: int32 [4, 64, 3], P(('grp', 'kv'), 'seq'), parts along dimension 0, may hold values from 0 to 31, as said below
- lengths: int32 [4], P(('grp', 'kv')), parts along dimension 0, may hold values from 8194 to 16384, as said below
Outputs:
- attended: bfloat16 [4, 64, 128], P(('grp', 'kv'), 'seq'), parts along dimension 0
There are 2 independent parts, one for each index of `grp`. A program takes and returns all parts, laid end to end along the dimension named above; each array names one. Nothing has to cross between parts.
Inputs may be any that keep to these rules, and one draw needn't show every extreme that they name: `picks`: each row of 3 holds distinct block numbers in ascending order; the last is the block that holds position lengths[b] - 1, the others lie before it. Position lengths[b] - 1 is never the first position of its block.
All inputs are finite; a program needn't handle non-finite values.
Results may differ from a plain program's by a relative error of at most 0.0046.
Values may be sent and summed in bfloat16 or wider, within the bound.
A program may use at most 64 MiB of HBM per device.

v0:
```python
import math
import jax
import jax.numpy as jnp
from jax import lax
from jax.sharding import PartitionSpec as P

BLOCK = 512
NEGATIVE = -1e30


def shards(queries, keys, values, picks, lengths):
    rows = queries.shape[0]
    head_dim = queries.shape[2]
    local_len = keys.shape[1]
    kv_heads = keys.shape[2]
    blocks_here = local_len // BLOCK
    seq_index = lax.axis_index("seq")
    all_queries, all_picks = (
        lax.all_gather(queries, "seq", axis=1, tiled=True),
        lax.all_gather(picks, "seq", axis=1, tiled=True),
    )
    heads = all_queries.shape[1]
    group = heads // kv_heads
    grouped = all_queries.reshape(rows, kv_heads, group, head_dim)
    scores = jnp.einsum("bkgd,btkd->bkgt", grouped, keys, preferred_element_type=jnp.float32) * (
        1.0 / math.sqrt(head_dim)
    )
    scores = scores.reshape(rows, kv_heads, group, blocks_here, BLOCK)
    block_ids = seq_index * blocks_here + jnp.arange(blocks_here, dtype=jnp.int32)
    chosen = jnp.any(all_picks[:, :, :, None] == block_ids[None, None, None, :], axis=2)
    chosen = chosen.reshape(rows, kv_heads, group, blocks_here)
    positions = block_ids[:, None] * BLOCK + jnp.arange(BLOCK, dtype=jnp.int32)[None, :]
    inside = positions[None, :, :] < lengths[:, None, None]
    live = jnp.logical_and(chosen[..., None], inside[:, None, None, :, :])
    masked = jnp.where(live, scores, -jnp.inf)
    any_live = jnp.any(live, axis=-1)
    safe_max = jnp.where(any_live, jnp.max(masked, axis=-1), NEGATIVE)
    weight = jnp.exp(masked - safe_max[..., None])
    block_total = jnp.sum(weight, axis=-1)
    rounded = weight.astype(jnp.bfloat16)
    blocked_values = values.reshape(rows, blocks_here, BLOCK, kv_heads, head_dim)
    block_out = jnp.einsum(
        "bkgnt,bntkd->bkgnd", rounded, blocked_values, preferred_element_type=jnp.float32
    )
    device_max = jnp.max(safe_max, axis=-1)
    coef = jnp.exp(safe_max - device_max[..., None])
    partial_out = jnp.sum(block_out * coef[..., None], axis=3).reshape(rows, heads, head_dim)
    partial_total = jnp.sum(block_total * coef, axis=-1).reshape(rows, heads)
    partial_max = device_max.reshape(rows, heads)
    came_out, came_max, came_total = (
        lax.all_to_all(partial_out[None], "seq", split_axis=2, concat_axis=0, tiled=True),
        lax.all_to_all(partial_max[None], "seq", split_axis=2, concat_axis=0, tiled=True),
        lax.all_to_all(partial_total[None], "seq", split_axis=2, concat_axis=0, tiled=True),
    )
    top = jnp.max(came_max, axis=0)
    rescale = jnp.exp(came_max - top[None])
    mine_out = jnp.sum(came_out * rescale[..., None], axis=0)
    mine_total = jnp.sum(came_total * rescale, axis=0)
    return (mine_out / mine_total[..., None]).astype(jnp.bfloat16)


def solution(mesh):
    return jax.shard_map(
        shards,
        mesh=mesh,
        in_specs=(
            P(("grp", "kv"), "seq", None),
            P(("grp", "kv"), "seq", None, None),
            P(("grp", "kv"), "seq", None, None),
            P(("grp", "kv"), "seq", None),
            P(("grp", "kv")),
        ),
        out_specs=P(("grp", "kv"), "seq", None),
        check_vma=False,
    )
```

profile of v0, /device:TPU:0, one launch (start us, length us, event | category | flops | bytes accessed | tf_op | source)
XLA Modules:
  0.0 97.5 jit_solution(2691425866918644044)
XLA Ops:
  0.7 0.8 copy.28
  1.4 28.1 %all_gather.7 = bf16[1,64,128]{2,1,0:T(8,128)(2,1)S(1)} all-gather(bf16[1,8,128]{2,1,0:T(8,128)(2,1)} %param.5), channel_id=1, replica_groups=mesh['grp'=2,'seq'=8,'kv'=2] {'seq'}, dimensions={1}, use_global_device_ids=true | all-gather | bytes 18432 | tf_op jit(solution)/shard_map/all_gather | solution.py:19
  29.5 30.6 %all_gather.6 = s32[1,64,3]{2,0,1:T(1,128)S(1)} all-gather(s32[1,8,3]{2,0,1:T(1,128)S(1)} %copy.28), channel_id=1, replica_groups=mesh['grp'=2,'seq'=8,'kv'=2] {'seq'}, dimensions={1}, use_global_device_ids=true | all-gather | bytes 864 | tf_op jit(solution)/shard_map/all_gather | solution.py:20
  60.1 0.1 compare_reduce_fusion
  60.2 0.1 and.40
  60.4 0.7 and_reduce_fusion
  61.1 3.4 %fusion.4 = f32[8,8,2048]{2,1,0:T(8,128)S(1)} fusion(bf16[2048,8,128]{2,1,0:T(8,128)(2,1)} %bitcast.31, bf16[1,64,128]{2,1,0:T(8,128)(2,1)S(1)} %all_gather.7), kind=kOutput, calls=%fused_computation.4 | convolution fusion | flops 33685504 | bytes 4734976 | tf_op jit(solution)/shard_map/bkgd,btkd->bkgt/dot_general | solution.py:25
  64.5 0.2 fusion.16
  64.8 0.7 broadcast_in_dim_reshape.13
  65.5 3.9 %all-to-all-start.1 = ((f32[1,1,64]{1,0,2:T(1,128)}), f32[1,1,64]{1,0,2:T(1,128)S(1)}, u32[]{:S(2)}, u32[]{:S(2)}) async-start(f32[1,1,64]{1,0,2:T(1,128)} %broadcast_in_dim_reshape.13), calls=%async_computation.1 | async-start | bytes 65536 | tf_op jit(solution)/shard_map/all_to_all | solution.py:52
  69.4 0.3 exponential_reduce_fusion
  69.7 0.7 broadcast_in_dim_reshape.14
  70.4 5.6 %all-to-all-done.1 = f32[1,1,64]{1,0,2:T(1,128)S(1)} async-done(((f32[1,1,64]{1,0,2:T(1,128)}), f32[1,1,64]{1,0,2:T(1,128)S(1)}, u32[]{:S(2)}, u32[]{:S(2)}) %all-to-all-start.1) | async-done | bytes 288 | tf_op jit(solution)/shard_map/all_to_all | solution.py:52
  76.1 3.3 %all-to-all-start.2 = ((f32[1,1,64]{1,0,2:T(1,128)}), f32[1,1,64]{1,0,2:T(1,128)S(1)}, u32[]{:S(2)}, u32[]{:S(2)}) async-start(f32[1,1,64]{1,0,2:T(1,128)} %broadcast_in_dim_reshape.14), calls=%async_computation.2 | async-start | bytes 65536 | tf_op jit(solution)/shard_map/all_to_all | solution.py:53
  79.4 4.1 %fusion.13 = f32[8,8,128]{2,1,0:T(8,128)} fusion(bf16[4,512,8,128]{3,2,1,0:T(8,128)(2,1)} %bitcast.34, f32[8,8,4,512]{3,1,2,0:T(8,128)S(1)} %bitcast.30, f32[8,8,4]{1,2,0:T(4,128)S(1)} %get-tuple-element.8, pred[4,512]{1,0:T(4,128)(4,1)S(1)} %add_compare_fusion, pred[8,8,4]{1,2,0:T(4,128)(4,1)S(1)} %copy.30, f32[8,8,4]{1,2,0:T(4,128)S(1)} %get-tuple-element.6), kind=kOutput, calls=%fused_computation.7 | convolution fusion | flops 34136064 | bytes 4755712 | tf_op jit(solution)/shard_map/bkgnt,bntkd->bkgnd/dot_general | solution.py:42
  83.5 0.6 reduce.12
  84.0 0.1 all_to_all.32
  84.1 0.1 all_to_all.35
  84.2 1.9 %all-to-all-done.2 = f32[1,1,64]{1,0,2:T(1,128)S(1)} async-done(((f32[1,1,64]{1,0,2:T(1,128)}), f32[1,1,64]{1,0,2:T(1,128)S(1)}, u32[]{:S(2)}, u32[]{:S(2)}) %all-to-all-start.2) | async-done | bytes 288 | tf_op jit(solution)/shard_map/all_to_all | solution.py:53
  86.0 4.1 %all-to-all-start = ((f32[1,1,64,128]{3,1,0,2:T(1,128)}), f32[1,1,64,128]{3,1,0,2:T(1,128)S(1)}, u32[]{:S(2)}, u32[]{:S(2)}) async-start(f32[1,1,64,128]{3,1,0,2:T(1,128)} %bitcast.10), calls=%async_computation | async-start | bytes 65536 | tf_op jit(solution)/shard_map/all_to_all | solution.py:51
  90.1 0.6 reduce.13
  90.7 0.1 all_to_all.34
  90.8 6.0 %all-to-all-done = f32[1,1,64,128]{3,1,0,2:T(1,128)S(1)} async-done(((f32[1,1,64,128]{3,1,0,2:T(1,128)}), f32[1,1,64,128]{3,1,0,2:T(1,128)S(1)}, u32[]{:S(2)}, u32[]{:S(2)}) %all-to-all-start) | async-done | bytes 32800 | tf_op jit(solution)/shard_map/all_to_all | solution.py:51
  96.9 0.7 fusion.22
  (11 shorter events, 0.3 us)
Async XLA Ops:
  65.5 10.5 %all-to-all-start.1 = ((f32[1,1,64]{1,0,2:T(1,128)}), f32[1,1,64]{1,0,2:T(1,128)S(1)}, u32[]{:S(2)}, u32[]{:S(2)}) async-start(f32[1,1,64]{1,0,2:T(1,128)} %broadcast_in_dim_reshape.13), calls=%async_computation.1 | async-start | bytes 65536 | tf_op jit(solution)/shard_map/all_to_all | solution.py:52
  76.1 10.0 %all-to-all-start.2 = ((f32[1,1,64]{1,0,2:T(1,128)}), f32[1,1,64]{1,0,2:T(1,128)S(1)}, u32[]{:S(2)}, u32[]{:S(2)}) async-start(f32[1,1,64]{1,0,2:T(1,128)} %broadcast_in_dim_reshape.14), calls=%async_computation.2 | async-start | bytes 65536 | tf_op jit(solution)/shard_map/all_to_all | solution.py:53
  86.0 10.8 %all-to-all-start = ((f32[1,1,64,128]{3,1,0,2:T(1,128)}), f32[1,1,64,128]{3,1,0,2:T(1,128)S(1)}, u32[]{:S(2)}, u32[]{:S(2)}) async-start(f32[1,1,64,128]{3,1,0,2:T(1,128)} %bitcast.10), calls=%async_computation | async-start | bytes 65536 | tf_op jit(solution)/shard_map/all_to_all | solution.py:51
where the time goes:
time: 98 us; the launch traced here: 97.5 us
  blocking collectives  58.7 us (60%)
  waiting for transfers between devices  13.5 us (14%)
  starting transfers between devices  11.3 us (12%)
  matrix products  7.44 us (8%)
  other arithmetic  3.38 us (3%)
  local copies, waits for them, and re-layouts  2.59 us (3%)
    all_gather x1, blocking collectives, shards(): lax.all_gather(picks, 'seq', axis=1, tiled=True)  30.6 us
    all_gather x1, blocking collectives, shards(): lax.all_gather(queries, 'seq', axis=1, tiled=True)  28.1 us
    all_to_all x1, waiting for transfers between devices, shards(): lax.all_to_all(partial_out[None], 'seq', split_axis=2, concat_axis=0, til...  5.99 us
    all_to_all x1, waiting for transfers between devices, shards(): lax.all_to_all(partial_max[None], 'seq', split_axis=2, concat_axis=0, til...  5.64 us
    all_to_all x1, starting transfers between devices, shards(): lax.all_to_all(partial_out[None], 'seq', split_axis=2, concat_axis=0, til...  4.09 us
    dot_general x1, matrix products, shards(): jnp.einsum('bkgnt,bntkd->bkgnd', rounded, blocked_values, preferred_eleme...  4.05 us
    all_to_all x1, starting transfers between devices, shards(): lax.all_to_all(partial_max[None], 'seq', split_axis=2, concat_axis=0, til...  3.86 us
    dot_general x1, matrix products, shards(): jnp.einsum('bkgd,btkd->bkgt', grouped, keys, preferred_element_type=jnp.f...  3.38 us
  transfers between devices with their start and end apart: 3, of which 3 were waited for; matrix products, arithmetic and copies ran while one was open for 6% of the time, Pallas kernels for 0%

commit v1 on v0

--- a/solution.py
+++ b/solution.py
@@ -1,3 +1,4 @@
+import functools
 import math
 import jax
 import jax.numpy as jnp
@@ -6,6 +7,19 @@
 
 BLOCK = 512
 NEGATIVE = -1e30
+
+
+def indices_arrange(x_part, row_axis):
+    long_array = jnp.concatenate(
+        lax.all_to_all(
+            jnp.stack(jnp.split(x_part, lax.psum(1, row_axis), axis=2), axis=0), row_axis, 0, 0
+        ),
+        axis=0,
+    )
+    return long_array
+
+
+recover_cube = functools.partial(indices_arrange, row_axis="seq")
 
 
 def shards(queries, keys, values, picks, lengths):
@@ -50,7 +64,7 @@
     came_out, came_max, came_total = (
         lax.all_to_all(partial_out[None], "seq", split_axis=2, concat_axis=0, tiled=True),
         lax.all_to_all(partial_max[None], "seq", split_axis=2, concat_axis=0, tiled=True),
-        lax.all_to_all(partial_total[None], "seq", split_axis=2, concat_axis=0, tiled=True),
+        recover_cube(partial_total[None]),
     )
     top = jnp.max(came_max, axis=0)
     rescale = jnp.exp(came_max - top[None])

time: 98 us -> 102 us (1.041)
  local copies, waits for them, and re-layouts: 2.59 us -> 6.72 us
  starting transfers between devices: 11.3 us -> 13.2 us
  waiting for transfers between devices: 13.5 us -> 12.3 us
    all_to_all x1, waiting for transfers between devices: 5.64 us -> 0.01 us  [shards(): lax.all_to_all(partial_max[None], 'seq', split_axis=2, concat_axis=0, til...]
    unnamed x1 -> x8, local copies, waits for them, and re-layouts: 0.76 us -> 5.02 us
    all_to_all x1, waiting for transfers between devices: 1.85 us -> 5.75 us  [indices_arrange(): lax.all_to_all(jnp.stack(jnp.split(x_part, lax.psum(1, row_axis), axis=2)...]
    all_to_all x1, starting transfers between devices: 3.33 us -> 6 us  [indices_arrange(): lax.all_to_all(jnp.stack(jnp.split(x_part, lax.psum(1, row_axis), axis=2)...]
  transfers between devices with their start and end apart: 3 -> 3, of which waited for: 3 -> 2; matrix products, arithmetic and copies ran while one was open for 6% -> 10% of each run, Pallas kernels for 0% -> 0%
where the time goes in v1:
time: 102 us
  blocking collectives  58.7 us (58%)
  starting transfers between devices  13.2 us (13%)
  waiting for transfers between devices  12.3 us (12%)
  matrix products  7.43 us (7%)
  local copies, waits for them, and re-layouts  6.72 us (7%)
  other arithmetic  2.83 us (3%)
    all_gather x1, blocking collectives, shards(): lax.all_gather(picks, 'seq', axis=1, tiled=True)  30.6 us
    all_gather x1, blocking collectives, shards(): lax.all_gather(queries, 'seq', axis=1, tiled=True)  28.1 us
    all_to_all x1, waiting for transfers between devices, shards(): lax.all_to_all(partial_out[None], 'seq', split_axis=2, concat_axis=0, til...  6.6 us
    all_to_all x1, starting transfers between devices, indices_arrange(): lax.all_to_all(jnp.stack(jnp.split(x_part, lax.psum(1, row_axis), axis=2)...  6 us
    all_to_all x1, waiting for transfers between devices, indices_arrange(): lax.all_to_all(jnp.stack(jnp.split(x_part, lax.psum(1, row_axis), axis=2)...  5.75 us
    unnamed x8, local copies, waits for them, and re-layouts  5.02 us
    dot_general x1, matrix products, shards(): jnp.einsum('bkgnt,bntkd->bkgnd', rounded, blocked_values, preferred_eleme...  4.05 us
    all_to_all x1, starting transfers between devices, shards(): lax.all_to_all(partial_max[None], 'seq', split_axis=2, concat_axis=0, til...  3.86 us
  transfers between devices with their start and end apart: 3, of which 2 were waited for; matrix products, arithmetic and copies ran while one was open for 10% of the time, Pallas kernels for 0%

profile of v1, /device:TPU:0, one launch (start us, length us, event | category | flops | bytes accessed | tf_op | source)
XLA Modules:
  0.0 101.9 jit_solution(16489853901849008188)
XLA Ops:
  0.7 0.8 copy.26
  1.4 28.1 %all_gather.7 = bf16[1,64,128]{2,1,0:T(8,128)(2,1)S(1)} all-gather(bf16[1,8,128]{2,1,0:T(8,128)(2,1)} %param.5), channel_id=1, replica_groups=mesh['grp'=2,'seq'=8,'kv'=2] {'seq'}, dimensions={1}, use_global_device_ids=true | all-gather | bytes 18432 | tf_op jit(solution)/shard_map/all_gather | solution.py:33
  29.5 30.6 %all_gather.6 = s32[1,64,3]{2,0,1:T(1,128)S(1)} all-gather(s32[1,8,3]{2,0,1:T(1,128)S(1)} %copy.26), channel_id=1, replica_groups=mesh['grp'=2,'seq'=8,'kv'=2] {'seq'}, dimensions={1}, use_global_device_ids=true | all-gather | bytes 864 | tf_op jit(solution)/shard_map/all_gather | solution.py:34
  60.4 0.7 and_reduce_fusion
  61.1 3.4 %fusion.4 = f32[8,8,2048]{2,1,0:T(8,128)S(1)} fusion(bf16[2048,8,128]{2,1,0:T(8,128)(2,1)} %bitcast.48, bf16[1,64,128]{2,1,0:T(8,128)(2,1)S(1)} %all_gather.7), kind=kOutput, calls=%fused_computation.4 | convolution fusion | flops 33685504 | bytes 4734976 | tf_op jit(solution)/shard_map/bkgd,btkd->bkgt/dot_general | solution.py:39
  64.5 0.2 fusion.16
  64.8 0.7 broadcast_in_dim_reshape.13
  65.5 3.9 %all-to-all-start.1 = ((f32[1,1,64]{1,0,2:T(1,128)}), f32[1,1,64]{1,0,2:T(1,128)S(1)}, u32[]{:S(2)}, u32[]{:S(2)}) async-start(f32[1,1,64]{1,0,2:T(1,128)} %broadcast_in_dim_reshape.13), calls=%async_computation.1 | async-start | bytes 65536 | tf_op jit(solution)/shard_map/all_to_all | solution.py:66
  69.4 0.3 exponential_reduce_fusion
  69.8 0.5 constant_dynamic-update-slice_fusion.7
  70.3 0.6 constant_dynamic-update-slice_fusion.6
  70.9 0.6 constant_dynamic-update-slice_fusion.5
  71.5 0.6 constant_dynamic-update-slice_fusion.4
  72.2 0.6 constant_dynamic-update-slice_fusion.3
  72.7 0.7 constant_dynamic-update-slice_fusion.2
  73.4 0.6 constant_dynamic-update-slice_fusion.1
  74.1 4.1 %fusion.13 = f32[8,8,128]{2,1,0:T(8,128)} fusion(bf16[4,512,8,128]{3,2,1,0:T(8,128)(2,1)} %bitcast.52, f32[8,8,4,512]{3,1,2,0:T(8,128)S(1)} %bitcast.47, f32[8,8,4]{1,2,0:T(4,128)S(1)} %get-tuple-element.8, pred[4,512]{1,0:T(4,128)(4,1)S(1)} %add_compare_fusion, pred[8,8,4]{1,2,0:T(4,128)(4,1)S(1)} %copy.28, f32[8,8,4]{1,2,0:T(4,128)S(1)} %get-tuple-element.6), kind=kOutput, calls=%fused_computation.7 | convolution fusion | flops 34136064 | bytes 4755712 | tf_op jit(solution)/shard_map/bkgnt,bntkd->bkgnd/dot_general | solution.py:56
  78.1 0.6 constant_dynamic-update-slice_fusion
  78.7 6.0 %all-to-all-start.2 = ((f32[8,1,1,8]{3,2,1,0:T(1,128)}), f32[8,1,1,8]{3,2,1,0:T(1,128)S(1)}, u32[]{:S(2)}, u32[]{:S(2)}) async-start(f32[8,1,1,8]{3,2,1,0:T(1,128)} %constant_dynamic-update-slice_fusion), calls=%async_computation.2 | async-start | bytes 8192 | tf_op jit(solution)/shard_map/all_to_all | solution.py:14
  84.7 0.6 reduce.12
  85.4 5.7 %all-to-all-done.2 = f32[8,1,1,8]{3,2,1,0:T(1,128)S(1)} async-done(((f32[8,1,1,8]{3,2,1,0:T(1,128)}), f32[8,1,1,8]{3,2,1,0:T(1,128)S(1)}, u32[]{:S(2)}, u32[]{:S(2)}) %all-to-all-start.2) | async-done | bytes 288 | tf_op jit(solution)/shard_map/all_to_all | solution.py:14
  91.2 3.3 %all-to-all-start = ((f32[1,1,64,128]{3,1,0,2:T(1,128)}), f32[1,1,64,128]{3,1,0,2:T(1,128)S(1)}, u32[]{:S(2)}, u32[]{:S(2)}) async-start(f32[1,1,64,128]{3,1,0,2:T(1,128)} %bitcast.10), calls=%async_computation | async-start | bytes 65536 | tf_op jit(solution)/shard_map/all_to_all | solution.py:65
  94.5 6.6 %all-to-all-done = f32[1,1,64,128]{3,1,0,2:T(1,128)S(1)} async-done(((f32[1,1,64,128]{3,1,0,2:T(1,128)}), f32[1,1,64,128]{3,1,0,2:T(1,128)S(1)}, u32[]{:S(2)}, u32[]{:S(2)}) %all-to-all-start) | async-done | bytes 32800 | tf_op jit(solution)/shard_map/all_to_all | solution.py:65
  101.2 0.7 fusion.22
  (17 shorter events, 0.8 us)
Async XLA Ops:
  65.5 13.2 %all-to-all-start.1 = ((f32[1,1,64]{1,0,2:T(1,128)}), f32[1,1,64]{1,0,2:T(1,128)S(1)}, u32[]{:S(2)}, u32[]{:S(2)}) async-start(f32[1,1,64]{1,0,2:T(1,128)} %broadcast_in_dim_reshape.13), calls=%async_computation.1 | async-start | bytes 65536 | tf_op jit(solution)/shard_map/all_to_all | solution.py:66
  78.7 12.5 %all-to-all-start.2 = ((f32[8,1,1,8]{3,2,1,0:T(1,128)}), f32[8,1,1,8]{3,2,1,0:T(1,128)S(1)}, u32[]{:S(2)}, u32[]{:S(2)}) async-start(f32[8,1,1,8]{3,2,1,0:T(1,128)} %constant_dynamic-update-slice_fusion), calls=%async_computation.2 | async-start | bytes 8192 | tf_op jit(solution)/shard_map/all_to_all | solution.py:14
  91.2 10.0 %all-to-all-start = ((f32[1,1,64,128]{3,1,0,2:T(1,128)}), f32[1,1,64,128]{3,1,0,2:T(1,128)S(1)}, u32[]{:S(2)}, u32[]{:S(2)}) async-start(f32[1,1,64,128]{3,1,0,2:T(1,128)} %bitcast.10), calls=%async_computation | async-start | bytes 65536 | tf_op jit(solution)/shard_map/all_to_all | solution.py:65
